TPU v7x, 32 devices: a whole 2x2x4 slice. The times are simulated.
32 devices in a mesh: gx: 8 (over z, x), gy: 4 (over y, core).
Axes of the slice: x: 2, y: 2, z: 4, core: 2. Of those that a mesh axis runs over, the one named last changes fastest.
Arguments:
- dense_grads: float32 [32, 256, 1024], P(('gx', 'gy')), may hold values from -6 to 6
- dense_param: float32 [256, 1024], P(('gx', 'gy')), may hold values from -6 to 6
- dense_acc: float32 [256, 1024], P(('gx', 'gy'))
- table: float32 [131072, 128], P(('gx', 'gy')), may hold values from -6 to 6
- row_acc: float32 [131072], P(('gx', 'gy'))
- touched: int32 [16384], P(('gx', 'gy')), may hold values from 0 to 4095, as said below
- emb_grads: float32 [16384, 128], P(('gx', 'gy'))
Outputs:
- new_dense: float32 [256, 1024], P(('gx', 'gy'))
- new_dense_acc: float32 [256, 1024], P(('gx', 'gy'))
- new_table: float32 [131072, 128], P(('gx', 'gy'))
- new_row_acc: float32 [131072], P(('gx', 'gy'))
Inputs may be any that keep to these rules, and one draw needn't show every extreme that they name: `touched`: within one device's 512 entries no row number repeats.
All inputs are finite; a program needn't handle non-finite values.
Results may differ from a plain program's by a relative error of at most 0.000022.
Values sent between devices are 32-bit elements; how exact they have to be, the bound alone decides.
A program may use at most 128 MiB of HBM per device.

v0:
```python
import jax
import jax.numpy as jnp
from jax import lax
from jax.sharding import PartitionSpec as P

learn_rate = 0.5
max_norm = 8.0
epsilon = 1e-10


def body(dense_grads, dense_param, dense_acc, table, row_acc, touched, emb_grads):
    shards = lax.axis_size(("gx", "gy"))
    local_grad = dense_grads[0]
    embed_square = jnp.sum(emb_grads * emb_grads)
    own_rows = dense_param.shape[0]
    summed, embed_total = lax.psum((local_grad, embed_square), ("gx", "gy"))
    mean_whole = summed / jnp.float32(shards)
    norm_sq = jnp.sum(mean_whole * mean_whole) + embed_total
    start = lax.axis_index(("gx", "gy")) * own_rows
    mean_grad = lax.dynamic_slice_in_dim(mean_whole, start, own_rows, 0)
    clip = jnp.minimum(jnp.float32(1.0), max_norm / (jnp.sqrt(norm_sq) + 1e-06))
    scaled = clip * mean_grad
    new_dense_acc = dense_acc + scaled * scaled
    new_dense = dense_param - learn_rate * scaled / (jnp.sqrt(new_dense_acc) + epsilon)
    row_grads = clip * emb_grads
    square_mean = jnp.mean(row_grads * row_grads, axis=1)
    updated_acc = row_acc[touched] + square_mean
    new_row_acc = row_acc.at[touched].set(updated_acc)
    updated_rows = (
        table[touched] - learn_rate * row_grads / (jnp.sqrt(updated_acc) + epsilon)[:, None]
    )
    new_table = table.at[touched].set(updated_rows)
    return (new_dense, new_dense_acc, new_table, new_row_acc)


def solution(mesh):
    return jax.shard_map(
        body,
        mesh=mesh,
        in_specs=(
            P(("gx", "gy"), None, None),
            P(("gx", "gy"), None),
            P(("gx", "gy"), None),
            P(("gx", "gy"), None),
            P(("gx", "gy")),
            P(("gx", "gy")),
            P(("gx", "gy"), None),
        ),
        out_specs=(
            P(("gx", "gy"), None),
            P(("gx", "gy"), None),
            P(("gx", "gy"), None),
            P(("gx", "gy")),
        ),
        check_vma=False,
    )
```

profile of v0, /device:TPU:0, one launch (start us, length us, event | category | flops | bytes accessed | tf_op | source)
XLA Modules:
  0.0 165.0 jit_solution(8833698111364106730)
XLA Ops:
  7.2 0.0 all-reduce.2.cloned.1.call-start
  7.2 0.7 copy.18
  7.9 0.0 all-reduce.2.cloned.1.call-update
  8.0 0.9 copy-done.3
  8.9 0.7 multiply_reduce_fusion.2
  9.5 42.3 %psum.15 = f32[]{:T(128)} all-reduce(f32[]{:T(128)} %multiply_reduce_fusion.2), channel_id=1, replica_groups=mesh['gx'=8,'gy'=4] {'gx','gy'}, use_global_device_ids=true, to_apply=%region_3.0 | all-reduce | flops 1 | bytes 8 | tf_op jit(solution)/shard_map/psum | solution.py:16
  51.9 0.0 copy-done.6
  51.9 3.1 %gather_fusion = f32[512]{0:T(512)S(1)} fusion(f32[4096]{0:T(1024)S(1)} %copy.18, s32[1024]{0:T(1024)S(1)} %pad_clamp_fusion), kind=kCustom, calls=%fused_computation.1 | custom fusion | bytes 6144 | tf_op jit(solution)/shard_map/gather | solution.py:27
  55.0 91.9 %all-reduce.2.cloned.1.call-done = f32[256,1024]{1,0:T(8,128)} async-done(((f32[256,1024]{1,0:T(8,128)}), f32[256,1024]{1,0:T(8,128)}) %all-reduce.2.cloned.1.call-update) | async-done | bytes 1048592 | tf_op jit(solution)/shard_map/psum | solution.py:16
  147.0 2.1 %multiply_reduce_fusion = (f32[]{:T(128)}, f32[256,1024]{1,0:T(8,128)S(1)}) fusion(f32[256,1024]{1,0:T(8,128)} %all-reduce.2.cloned.1.call-done), kind=kLoop, calls=%fused_computation.4 | loop fusion | flops 786431 | bytes 2097156 | tf_op jit(solution)/shard_map/reduce_sum | solution.py:18
  150.5 0.1 multiply_reduce_fusion.1
  150.6 0.0 copy-start.2
  150.6 2.5 %scatter_fusion = f32[4096]{0:T(1024)S(1)} fusion(f32[4096]{0:T(1024)S(1)} %copy.18, s32[512]{0:T(512)S(1)} %compare_select_fusion, f32[512]{0:T(512)S(1)} %get-tuple-element.5), kind=kCustom, calls=%fused_computation.3 | custom fusion | bytes 8192 | tf_op jit(solution)/shard_map/scatter | solution.py:28
  153.1 0.0 copy-start
  153.1 0.0 copy-done.2
  153.1 0.0 copy-start.4
  153.2 0.0 copy-start.5
  153.2 3.6 %scatter_custom_fusion = f32[4096,128]{1,0:T(8,128)S(1)} fusion(f32[4096,128]{1,0:T(8,128)S(1)} %copy-done.2, s32[512]{0:T(512)S(1)} %compare_select_fusion, f32[512,128]{1,0:T(8,128)S(1)} %copy-done.3, f32[512]{0:T(512)S(1)} %get-tuple-element.4, f32[]{:T(128)} %constant.14.clone.1, f32[]{:T(128)S(6)} %min_shard_map.3, s32[1024]{0:T(1024)S(1)} %pad_clamp_fusion), kind=kCustom, calls=%fused_computation.6 | custom fusion | flops 262144 | bytes 4462600 | tf_op jit(solution)/shard_map/scatter | solution.py:32
  156.8 0.0 copy-done
  156.8 0.0 copy-start.1
  156.8 0.0 copy-done.4
  156.8 0.0 copy-done.5
  156.8 0.8 divide_subtract_fusion
  157.6 0.5 copy-done.1
  (5 shorter events, 0.0 us)
Async XLA Ops:
  7.2 139.8 %all-reduce.2.cloned.1.call-start = ((), (), s32[]{:S(2)}) async-start(), calls=%async_computation | async-start | bytes 2097152 | tf_op jit(solution)/shard_map/psum | solution.py:16
  7.9 0.9 copy-start.3
  7.9 43.9 %copy-start.6 = (s32[512]{0:T(512)S(1)}, s32[512]{0:T(512)}, u32[]{:S(2)}) copy-start(s32[512]{0:T(512)} %param.12) | copy-start | bytes 6148
  150.6 2.5 %copy-start.2 = (f32[4096,128]{1,0:T(8,128)S(1)}, f32[4096,128]{1,0:T(8,128)}, u32[]{:S(2)}) copy-start(f32[4096,128]{1,0:T(8,128)} %param.10) | copy-start | bytes 6291460
  153.1 3.7 %copy-start = (f32[4096]{0:T(1024)}, f32[4096]{0:T(1024)S(1)}, u32[]{:S(2)}) copy-start(f32[4096]{0:T(1024)S(1)} %scatter_fusion) | copy-start | bytes 49156
  153.1 3.7 %copy-start.4 = (f32[8,1024]{1,0:T(8,128)S(1)}, f32[8,1024]{1,0:T(8,128)}, u32[]{:S(2)}) copy-start(f32[8,1024]{1,0:T(8,128)} %param.8) | copy-start | bytes 98308
  153.2 3.7 %copy-start.5 = (f32[8,1024]{1,0:T(8,128)S(1)}, f32[8,1024]{1,0:T(8,128)}, u32[]{:S(2)}) copy-start(f32[8,1024]{1,0:T(8,128)} %param.9) | copy-start | bytes 98308
  156.8 1.3 copy-start.1
Sparse Core Ops, SparseCore 0:
  13.2 133.7 all-reduce.1
where the time goes:
time: 165 us
  waiting for transfers between devices  92 us (56%)
  blocking collectives  42.3 us (26%)
  between operations  15.5 us (9%)
  local copies, waits for them, and re-layouts  7.84 us (5%)
  other arithmetic  7.32 us (4%)
    psum x1, waiting for transfers between devices, body(): summed, embed_total = lax.psum((local_grad, embed_square), ('gx', 'gy'))  91.9 us
    psum x1, blocking collectives, body(): summed, embed_total = lax.psum((local_grad, embed_square), ('gx', 'gy'))  42.3 us
    scatter x1, other arithmetic, body(): new_table = table.at[touched].set(updated_rows)  3.6 us
  transfers between devices with their start and end apart: 1, of which 1 were waited for; matrix products, arithmetic and copies ran while one was open for 2% of the time, Pallas kernels for 0%

commit v1 on v0

v1 whole, which is shorter than its diff:
```python
import functools

import jax
import jax.numpy as jnp
from jax import lax
from jax.experimental import pallas as pl
from jax.experimental.pallas import tpu as pltpu
from jax.sharding import PartitionSpec as P

learn_rate = 0.5
max_norm = 8.0
epsilon = 1e-10

MESH = pl.DeviceIdType.MESH
LANES = 128
UNROLL = 16


def flip(index, mask, size):
    result, bit = 0, 1
    while bit < size:
        digit = (index // bit) % 2
        result = result + bit * ((1 - digit) if mask & bit else digit)
        bit *= 2
    return result


def exchange(
    dims,
    grads,
    emb,
    racc,
    touched,
    mean_out,
    clip_out,
    lane_out,
    acc_out,
    own,
    pair_in,
    sums,
    plane_in,
    line_send,
    line_in,
    norms,
    load_sem,
    pair_send_sem,
    pair_sem,
    plane_send_sem,
    plane_sem,
    line_send_sem,
    line_sem,
    norm_send_sem,
    norm_sem,
):
    slows, fasts, ys, cores = dims
    gx, gy = lax.axis_index("gx"), lax.axis_index("gy")
    slow, fast = gx // fasts, gx % fasts
    y, core = gy // cores, gy % cores
    other = 1 - core
    plane = [(a, b) for a in reversed(range(fasts)) for b in reversed(range(ys)) if a or b]
    order = list(reversed(range(slows)))

    loads = {}
    for k in order:
        loads[k] = pltpu.make_async_copy(grads.at[flip(slow, k, slows)], own.at[k], load_sem.at[k])
        loads[k].start()

    barrier = pltpu.get_barrier_semaphore()
    greet = [(gx, y * cores + other)]
    for a, b in plane:
        greet.append((slow * fasts + flip(fast, a, fasts), flip(y, b, ys) * cores + core))
    for k in range(1, slows):
        greet.append((flip(slow, k, slows) * fasts + fast, gy))
    for device in greet:
        pl.semaphore_signal(barrier, inc=1, device_id=device, device_id_type=MESH)
    pl.semaphore_wait(barrier, len(greet))

    pair = {}
    for k in order:
        loads[k].wait()
        pair[k] = pltpu.make_async_remote_copy(
            src_ref=own.at[k, :, :, other],
            dst_ref=pair_in.at[k],
            send_sem=pair_send_sem.at[k],
            recv_sem=pair_sem.at[k],
            device_id=(gx, y * cores + other),
            device_id_type=MESH,
        )
        pair[k].start()

    across = {}
    for k in order:
        pair[k].wait_recv()
        for a in range(fasts):
            for b in range(ys):
                f, v = flip(fast, a, fasts), flip(y, b, ys)
                sums[k, a * ys + b] = own[k, f, v, core] + pair_in[k, f, v]
        for a, b in plane:
            q = a * ys + b
            across[k, q] = pltpu.make_async_remote_copy(
                src_ref=sums.at[k, q],
                dst_ref=plane_in.at[k, q],
                send_sem=plane_send_sem.at[k, q],
                recv_sem=plane_sem.at[k, q],
                device_id=(slow * fasts + flip(fast, a, fasts), flip(y, b, ys) * cores + core),
                device_id_type=MESH,
            )
            across[k, q].start()

    lane = lax.broadcasted_iota(jnp.int32, (1, LANES), 1)

    def gather(step, carry):
        for i in range(UNROLL):
            t = step * UNROLL + i
            row = touched[t]
            here = lane == row % LANES
            lane_out[pl.ds(t, 1), :] = jnp.where(here, 1.0, 0.0)
            acc_out[pl.ds(t, 1), :] = jnp.where(here, racc[pl.ds(row // LANES, 1), :], 0.0)
        return carry

    lax.fori_loop(0, touched.shape[0] // UNROLL, gather, 0)
    values = emb[...]
    emb_square = jnp.sum(values * values, axis=0, keepdims=True)

    def plane_total(k):
        total = sums[k, 0]
        for a, b in plane:
            across[k, a * ys + b].wait_recv()
            total = total + plane_in[k, a * ys + b]
        return total

    line = {}
    for k in order[:-1]:
        line_send[k] = plane_total(k)
        line[k] = pltpu.make_async_remote_copy(
            src_ref=line_send.at[k],
            dst_ref=line_in.at[k],
            send_sem=line_send_sem.at[k],
            recv_sem=line_sem.at[k],
            device_id=(flip(slow, k, slows) * fasts + fast, gy),
            device_id_type=MESH,
        )
        line[k].start()
    total = plane_total(0)
    for k in order[:-1]:
        line[k].wait_recv()
        total = total + line_in[k]

    shards = slows * fasts * ys * cores
    mean = total / jnp.float32(shards)
    mean_out[...] = mean
    square = mean * mean
    partial = square[:, :LANES]
    for start in range(LANES, square.shape[1], LANES):
        partial = partial + square[:, start : start + LANES]
    norms[0] = jnp.sum(partial, axis=0, keepdims=True) + emb_square

    width, height = slows * fasts, ys * cores
    spread = []
    for k in reversed(range(1, shards)):
        spread.append(
            pltpu.make_async_remote_copy(
                src_ref=norms.at[0],
                dst_ref=norms.at[k],
                send_sem=norm_send_sem,
                recv_sem=norm_sem,
                device_id=(flip(gx, k // height, width), flip(gy, k % height, height)),
                device_id_type=MESH,
            )
        )
        spread[-1].start()
    everyone = pltpu.make_async_copy(
        norms.at[pl.ds(1, shards - 1)], norms.at[pl.ds(1, shards - 1)], norm_sem
    )
    everyone.wait()
    norm_sq = jnp.sum(jnp.sum(norms[...], axis=0), axis=1, keepdims=True)
    clip = jnp.minimum(jnp.float32(1.0), max_norm / (jnp.sqrt(norm_sq) + 1e-06))
    clip_out[...] = jnp.broadcast_to(clip, clip_out.shape)

    for k in order:
        pair[k].wait_send()
    for copy in list(across.values()) + list(line.values()):
        copy.wait_send()
    pltpu.make_async_copy(
        norms.at[pl.ds(1, shards - 1)], norms.at[pl.ds(1, shards - 1)], norm_send_sem
    ).wait()


def update(
    table,
    touched,
    touched_rows,
    clip_ref,
    mean,
    dense_param,
    dense_acc,
    emb,
    lane_hot,
    acc_at,
    racc,
    new_table,
    new_dense,
    new_dense_acc,
    new_racc,
    held,
    change,
    sem,
):
    load = pltpu.make_async_copy(table, held, sem)
    load.start()
    clip = clip_ref[:, :1]
    scaled = clip * mean[...]
    acc = dense_acc[...] + scaled * scaled
    new_dense_acc[...] = acc
    new_dense[...] = dense_param[...] - learn_rate * scaled / (jnp.sqrt(acc) + epsilon)

    row_grads = clip * emb[...]
    width = row_grads.shape[1]
    square_mean = jnp.sum(row_grads * row_grads, axis=1, keepdims=True) / jnp.float32(width)
    updated_acc = jnp.sum(acc_at[...], axis=1, keepdims=True) + square_mean
    change[...] = learn_rate * row_grads / (jnp.sqrt(updated_acc) + epsilon)

    placed = lane_hot[...] * square_mean
    groups = lax.broadcasted_iota(jnp.int32, racc.shape, 0)
    added = racc[...]
    for part in range(touched_rows.shape[0]):
        rows = touched_rows[part : part + 1, :]
        hot = jnp.where(groups == rows // LANES, 1.0, 0.0)
        added = added + jnp.dot(
            hot,
            placed[part * LANES : (part + 1) * LANES],
            precision=lax.Precision.HIGHEST,
            preferred_element_type=jnp.float32,
        )
    new_racc[...] = added
    load.wait()

    def scatter(step, carry):
        base = step * UNROLL
        rows = [touched[base + i] for i in range(UNROLL)]
        fresh = [held[pl.ds(rows[i], 1), :] - change[pl.ds(base + i, 1), :] for i in range(UNROLL)]
        for i in range(UNROLL):
            held[pl.ds(rows[i], 1), :] = fresh[i]
        return carry

    lax.fori_loop(0, touched.shape[0] // UNROLL, scatter, 0)
    store = pltpu.make_async_copy(held, new_table, sem)
    store.start()
    store.wait()


def body(dims, dense_grads, dense_param, dense_acc, table, row_acc, touched, emb_grads):
    slows, fasts, ys, cores = dims
    shards = slows * fasts * ys * cores
    rows, wide = dense_param.shape
    f32 = jnp.float32
    count, width = emb_grads.shape
    grads = dense_grads.reshape(slows, fasts, ys, cores, rows, wide)
    racc = row_acc.reshape(-1, LANES)
    touched_rows = touched.reshape(-1, LANES)
    vmem = pl.BlockSpec(memory_space=pltpu.VMEM)
    smem = pl.BlockSpec(memory_space=pltpu.SMEM)
    hbm = pl.BlockSpec(memory_space=pl.ANY)
    quad = fasts * ys
    dma = pltpu.SemaphoreType.DMA
    block = jax.ShapeDtypeStruct((rows, wide), f32)
    per_row = jax.ShapeDtypeStruct((count, LANES), f32)
    mean, clip, lane_hot, acc_at = pl.pallas_call(
        functools.partial(exchange, dims),
        name="exchange",
        out_shape=(block, jax.ShapeDtypeStruct((1, LANES), f32), per_row, per_row),
        in_specs=[hbm, vmem, vmem, smem],
        out_specs=(vmem,) * 4,
        scratch_shapes=[
            pltpu.VMEM((slows, fasts, ys, cores, rows, wide), f32),
            pltpu.VMEM((slows, fasts, ys, rows, wide), f32),
            pltpu.VMEM((slows, quad, rows, wide), f32),
            pltpu.VMEM((slows, quad, rows, wide), f32),
            pltpu.VMEM((slows, rows, wide), f32),
            pltpu.VMEM((slows, rows, wide), f32),
            pltpu.VMEM((shards, 1, LANES), f32),
            dma((slows,)),
            dma((slows,)),
            dma((slows,)),
            dma((slows, quad)),
            dma((slows, quad)),
            dma((slows,)),
            dma((slows,)),
            dma,
            dma,
        ],
        compiler_params=pltpu.CompilerParams(collective_id=0, has_side_effects=True),
    )(grads, emb_grads, racc, touched)
    new_table, new_dense, new_dense_acc, new_racc = pl.pallas_call(
        update,
        name="update",
        out_shape=(
            jax.ShapeDtypeStruct(table.shape, f32),
            block,
            block,
            jax.ShapeDtypeStruct(racc.shape, f32),
        ),
        in_specs=[hbm, smem] + [vmem] * 9,
        out_specs=(hbm, vmem, vmem, vmem),
        scratch_shapes=[
            pltpu.VMEM(table.shape, f32),
            pltpu.VMEM((count, width), f32),
            dma,
        ],
    )(table, touched, touched_rows, clip, mean, dense_param, dense_acc, emb_grads, lane_hot, acc_at, racc)
    return new_dense, new_dense_acc, new_table, new_racc.reshape(-1)


def solution(mesh):
    wide, high = mesh.shape["gx"], mesh.shape["gy"]
    dims = (wide // 2, 2, high // 2, 2)
    return jax.shard_map(
        functools.partial(body, dims),
        mesh=mesh,
        in_specs=(
            P(("gx", "gy"), None, None),
            P(("gx", "gy"), None),
            P(("gx", "gy"), None),
            P(("gx", "gy"), None),
            P(("gx", "gy")),
            P(("gx", "gy")),
            P(("gx", "gy"), None),
        ),
        out_specs=(
            P(("gx", "gy"), None),
            P(("gx", "gy"), None),
            P(("gx", "gy"), None),
            P(("gx", "gy")),
        ),
        check_vma=False,
    )
```

time: 165 us -> 29.1 us (0.18)
  waiting for transfers between devices: 92 us -> 0 us
  blocking collectives: 42.3 us -> 0 us
  Pallas kernels: 0 us -> 28.3 us
  between operations: 15.5 us -> 0.64 us
  local copies, waits for them, and re-layouts: 7.84 us -> 0 us
  other arithmetic: 7.32 us -> 0 us
    psum x1 -> x0, waiting for transfers between devices: 91.9 us -> none  [body(): summed, embed_total = lax.psum((local_grad, embed_square), ('gx', 'gy'))]
    psum x1 -> x0, blocking collectives: 42.3 us -> none  [body(): summed, embed_total = lax.psum((local_grad, embed_square), ('gx', 'gy'))]
    pallas_call x0 -> x2, Pallas kernels: none -> 28.3 us  [the longest x1 22.7 us: body(): pl.pallas_call(functools.partial(exchange, dims), name='exchange', out_sh...]
    scatter x1 -> x0, other arithmetic: 3.6 us -> none  [body(): new_table = table.at[touched].set(updated_rows)]
    gather x1 -> x0, local copies, waits for them, and re-layouts: 3.14 us -> none  [body(): updated_acc = row_acc[touched] + square_mean]
    reduce_sum x3 -> x0, other arithmetic: 2.92 us -> none  [the longest x1 2.11 us: body(): norm_sq = jnp.sum(mean_whole * mean_whole) + embed_total]
    scatter x1 -> x0, local copies, waits for them, and re-layouts: 2.48 us -> none  [body(): new_row_acc = row_acc.at[touched].set(updated_acc)]
    unnamed x15 -> x0, local copies, waits for them, and re-layouts: 2.22 us -> none
  transfers between devices with their start and end apart: 1 -> 0, of which waited for: 1 -> 0; matrix products, arithmetic and copies ran while one was open for 2% -> 0% of each run, Pallas kernels for 0% -> 0%
where the time goes in v1:
time: 29.1 us; the launch traced here: 28.9 us
  Pallas kernels  28.3 us (97%)
  between operations  0.64 us (2%)
    pallas_call x1, Pallas kernels, body(): pl.pallas_call(functools.partial(exchange, dims), name='exchange', out_sh...  22.7 us
    pallas_call x1, Pallas kernels, body(): pl.pallas_call(update, name='update', out_shape=(jax.ShapeDtypeStruct(tab...  5.56 us

profile of v1, /device:TPU:0, one launch (start us, length us, event | category | flops | bytes accessed | tf_op | source)
XLA Modules:
  0.0 28.9 jit_solution(14948009262113397559)
XLA Ops:
  0.6 22.7 %exchange.1 = (f32[8,1024]{1,0:T(8,128)}, f32[1,128]{1,0:T(1,128)}, f32[512,128]{1,0:T(8,128)}, f32[512,128]{1,0:T(8,128)}) custom-call(f32[4,2,2,2,8,1024]{5,4,3,2,1,0:T(8,128)} %bitcast.4, f32[512,128]{1,0:T(8,128)} %emb.3, f32[32,128]{1,0:T(8,128)} %bitcast.5, s32[512]{0:T(512)} %touched.3), custom_call_target="tpu_custom_call" | custom-call | tf_op jit(solution)/shard_map/exchange/pallas_call | solution.py:268
  23.3 5.6 %update.1 = (f32[4096,128]{1,0:T(8,128)}, f32[8,1024]{1,0:T(8,128)}, f32[8,1024]{1,0:T(8,128)}, f32[32,128]{1,0:T(8,128)}) custom-call(f32[4096,128]{1,0:T(8,128)} %table.1, s32[512]{0:T(512)} %touched.3, s32[4,128]{1,0:T(4,128)} %bitcast.7, f32[1,128]{1,0:T(1,128)} %get-tuple-element.12.clip_ref, f32[8,1024]{1,0:T(8,128)} %get-tuple-element.13.mean, ...), custom_call_target="tpu_custom_call" | custom-call | tf_op jit(solution)/shard_map/update/pallas_call | solution.py:294

commit v2 on v1

--- a/solution.py
+++ b/solution.py
@@ -28,13 +28,21 @@
 def exchange(
     dims,
     grads,
-    emb,
-    racc,
-    touched,
+    emb_hbm,
+    racc_hbm,
+    touched_hbm,
+    table_hbm,
+    param_hbm,
+    dense_acc_hbm,
     mean_out,
     clip_out,
     lane_out,
     acc_out,
+    table_out,
+    emb,
+    racc,
+    param_out,
+    dense_acc_out,
     own,
     pair_in,
     sums,
@@ -42,6 +50,7 @@
     line_send,
     line_in,
     norms,
+    touched,
     load_sem,
     pair_send_sem,
     pair_sem,
@@ -51,6 +60,7 @@
     line_sem,
     norm_send_sem,
     norm_sem,
+    side_sem,
 ):
     slows, fasts, ys, cores = dims
     gx, gy = lax.axis_index("gx"), lax.axis_index("gy")
@@ -64,6 +74,18 @@
     for k in order:
         loads[k] = pltpu.make_async_copy(grads.at[flip(slow, k, slows)], own.at[k], load_sem.at[k])
         loads[k].start()
+    sides = []
+    held = (
+        (touched_hbm, touched),
+        (racc_hbm, racc),
+        (emb_hbm, emb),
+        (param_hbm, param_out),
+        (dense_acc_hbm, dense_acc_out),
+        (table_hbm, table_out),
+    )
+    for n, (source, target) in enumerate(held):
+        sides.append(pltpu.make_async_copy(source, target, side_sem.at[n]))
+        sides[-1].start()
 
     barrier = pltpu.get_barrier_semaphore()
     greet = [(gx, y * cores + other)]
@@ -107,6 +129,8 @@
             )
             across[k, q].start()
 
+    for side in sides[:3]:
+        side.wait()
     lane = lax.broadcasted_iota(jnp.int32, (1, LANES), 1)
 
     def gather(step, carry):
@@ -177,6 +201,8 @@
     clip = jnp.minimum(jnp.float32(1.0), max_norm / (jnp.sqrt(norm_sq) + 1e-06))
     clip_out[...] = jnp.broadcast_to(clip, clip_out.shape)
 
+    for side in sides[3:]:
+        side.wait()
     for k in order:
         pair[k].wait_send()
     for copy in list(across.values()) + list(line.values()):
@@ -198,43 +224,40 @@
     lane_hot,
     acc_at,
     racc,
+    held,
     new_table,
     new_dense,
     new_dense_acc,
     new_racc,
-    held,
     change,
-    sem,
+    dense_v,
+    acc_v,
+    racc_v,
+    sems,
 ):
-    load = pltpu.make_async_copy(table, held, sem)
-    load.start()
     clip = clip_ref[:, :1]
-    scaled = clip * mean[...]
-    acc = dense_acc[...] + scaled * scaled
-    new_dense_acc[...] = acc
-    new_dense[...] = dense_param[...] - learn_rate * scaled / (jnp.sqrt(acc) + epsilon)
-
-    row_grads = clip * emb[...]
-    width = row_grads.shape[1]
-    square_mean = jnp.sum(row_grads * row_grads, axis=1, keepdims=True) / jnp.float32(width)
-    updated_acc = jnp.sum(acc_at[...], axis=1, keepdims=True) + square_mean
-    change[...] = learn_rate * row_grads / (jnp.sqrt(updated_acc) + epsilon)
-
-    placed = lane_hot[...] * square_mean
-    groups = lax.broadcasted_iota(jnp.int32, racc.shape, 0)
-    added = racc[...]
-    for part in range(touched_rows.shape[0]):
-        rows = touched_rows[part : part + 1, :]
-        hot = jnp.where(groups == rows // LANES, 1.0, 0.0)
-        added = added + jnp.dot(
+    count, width = emb.shape
+
+    def prepare(step, carry):
+        part = pl.ds(pl.multiple_of(step * LANES, LANES), LANES)
+        row_grads = clip * emb[part, :]
+        square_mean = jnp.sum(row_grads * row_grads, axis=1, keepdims=True) / jnp.float32(width)
+        updated_acc = jnp.sum(acc_at[part, :], axis=1, keepdims=True) + square_mean
+        change[part, :] = learn_rate * row_grads / (jnp.sqrt(updated_acc) + epsilon)
+        placed = lane_hot[part, :] * square_mean
+        hot = jnp.where(groups == touched_rows[pl.ds(step, 1), :] // LANES, 1.0, 0.0)
+        racc_v[...] += jnp.dot(
             hot,
-            placed[part * LANES : (part + 1) * LANES],
+            placed,
             precision=lax.Precision.HIGHEST,
             preferred_element_type=jnp.float32,
         )
-    new_racc[...] = added
-    load.wait()
-
+        return carry
+
+    groups = lax.broadcasted_iota(jnp.int32, racc.shape, 0)
+    racc_v[...] = racc[...]
+    for step in range(count // LANES):
+        prepare(step, 0)
     def scatter(step, carry):
         base = step * UNROLL
         rows = [touched[base + i] for i in range(UNROLL)]
@@ -244,9 +267,19 @@
         return carry
 
     lax.fori_loop(0, touched.shape[0] // UNROLL, scatter, 0)
-    store = pltpu.make_async_copy(held, new_table, sem)
-    store.start()
-    store.wait()
+    stores = [pltpu.make_async_copy(held, new_table, sems.at[0])]
+    stores[0].start()
+
+    scaled = clip * mean[...]
+    acc = dense_acc[...] + scaled * scaled
+    acc_v[...] = acc
+    dense_v[...] = dense_param[...] - learn_rate * scaled / (jnp.sqrt(acc) + epsilon)
+    pairs = ((racc_v, new_racc), (acc_v, new_dense_acc), (dense_v, new_dense))
+    for n, (source, target) in enumerate(pairs):
+        stores.append(pltpu.make_async_copy(source, target, sems.at[n + 1]))
+        stores[-1].start()
+    for store in stores:
+        store.wait()
 
 
 def body(dims, dense_grads, dense_param, dense_acc, table, row_acc, touched, emb_grads):
@@ -265,12 +298,14 @@
     dma = pltpu.SemaphoreType.DMA
     block = jax.ShapeDtypeStruct((rows, wide), f32)
     per_row = jax.ShapeDtypeStruct((count, LANES), f32)
-    mean, clip, lane_hot, acc_at = pl.pallas_call(
+    own = (table, emb_grads, racc, dense_param, dense_acc)
+    mean, clip, lane_hot, acc_at, held, emb, racc, param, acc = pl.pallas_call(
         functools.partial(exchange, dims),
         name="exchange",
-        out_shape=(block, jax.ShapeDtypeStruct((1, LANES), f32), per_row, per_row),
-        in_specs=[hbm, vmem, vmem, smem],
-        out_specs=(vmem,) * 4,
+        out_shape=(block, jax.ShapeDtypeStruct((1, LANES), f32), per_row, per_row)
+        + tuple(jax.ShapeDtypeStruct(a.shape, f32) for a in own),
+        in_specs=[hbm] * 7,
+        out_specs=(vmem,) * 9,
         scratch_shapes=[
             pltpu.VMEM((slows, fasts, ys, cores, rows, wide), f32),
             pltpu.VMEM((slows, fasts, ys, rows, wide), f32),
@@ -279,6 +314,7 @@
             pltpu.VMEM((slows, rows, wide), f32),
             pltpu.VMEM((slows, rows, wide), f32),
             pltpu.VMEM((shards, 1, LANES), f32),
+            pltpu.SMEM((count,), jnp.int32),
             dma((slows,)),
             dma((slows,)),
             dma((slows,)),
@@ -288,26 +324,36 @@
             dma((slows,)),
             dma,
             dma,
+            dma((6,)),
         ],
-        compiler_params=pltpu.CompilerParams(collective_id=0, has_side_effects=True),
-    )(grads, emb_grads, racc, touched)
-    new_table, new_dense, new_dense_acc, new_racc = pl.pallas_call(
+        compiler_params=pltpu.CompilerParams(
+            collective_id=0, has_side_effects=True, vmem_limit_bytes=49 << 20
+        ),
+    )(grads, emb_grads, racc, touched, table, dense_param, dense_acc)
+    _, new_table, new_dense, new_dense_acc, new_racc = pl.pallas_call(
         update,
         name="update",
         out_shape=(
             jax.ShapeDtypeStruct(table.shape, f32),
+            jax.ShapeDtypeStruct(table.shape, f32),
             block,
             block,
             jax.ShapeDtypeStruct(racc.shape, f32),
         ),
-        in_specs=[hbm, smem] + [vmem] * 9,
-        out_specs=(hbm, vmem, vmem, vmem),
+        in_specs=[vmem, smem] + [vmem] * 9,
+        out_specs=(vmem,) + (hbm,) * 4,
+        input_output_aliases={0: 0},
         scratch_shapes=[
-            pltpu.VMEM(table.shape, f32),
             pltpu.VMEM((count, width), f32),
-            dma,
+            pltpu.VMEM((rows, wide), f32),
+            pltpu.VMEM((rows, wide), f32),
+            pltpu.VMEM(racc.shape, f32),
+            dma((4,)),
         ],
-    )(table, touched, touched_rows, clip, mean, dense_param, dense_acc, emb_grads, lane_hot, acc_at, racc)
+        compiler_params=pltpu.CompilerParams(
+            vmem_limit_bytes=2 * table.size * 4 + 8 * count * LANES * 4 + (4 << 20)
+        ),
+    )(held, touched, touched_rows, clip, mean, param, acc, emb, lane_hot, acc_at, racc)
     return new_dense, new_dense_acc, new_table, new_racc.reshape(-1)
 
 

time: 29.1 us -> 30.7 us (1.055)
  local copies, waits for them, and re-layouts: 0 us -> 5.08 us
  Pallas kernels: 28.3 us -> 24.5 us
    unnamed x0 -> x12, local copies, waits for them, and re-layouts: none -> 5.08 us
    pallas_call x1, Pallas kernels: 5.56 us -> 3.34 us  [body(): pl.pallas_call(update, name='update', out_shape=(jax.ShapeDtypeStruct(tab...]
    pallas_call x1, Pallas kernels: 22.7 us -> 21.2 us  [body(): pl.pallas_call(functools.partial(exchange, dims), name='exchange', out_sh...]
where the time goes in v2:
time: 30.7 us; the launch traced here: 30.3 us
  Pallas kernels  24.5 us (80%)
  local copies, waits for them, and re-layouts  5.08 us (17%)
  between operations  0.65 us (2%)
    pallas_call x1, Pallas kernels, body(): pl.pallas_call(functools.partial(exchange, dims), name='exchange', out_sh...  21.2 us
    unnamed x12, local copies, waits for them, and re-layouts  5.08 us
    pallas_call x1, Pallas kernels, body(): pl.pallas_call(update, name='update', out_shape=(jax.ShapeDtypeStruct(tab...  3.34 us

profile of v2, /device:TPU:0, one launch (start us, length us, event | category | flops | bytes accessed | tf_op | source)
XLA Modules:
  0.0 30.3 jit_solution(17740264617166728036)
XLA Ops:
  0.6 0.0 copy-start
  0.6 1.2 %copy-done = f32[1,256,1024]{2,1,0:T(8,128)S(1)} copy-done((f32[1,256,1024]{2,1,0:T(8,128)S(1)}, f32[1,256,1024]{2,1,0:T(8,128)}, u32[]{:S(2)}) %copy-start) | copy-done | bytes 1048600
  1.9 0.0 copy-start.1
  1.9 0.9 %copy-done.1 = f32[512,128]{1,0:T(8,128)S(1)} copy-done((f32[512,128]{1,0:T(8,128)S(1)}, f32[512,128]{1,0:T(8,128)}, u32[]{:S(2)}) %copy-start.1) | copy-done | bytes 262168
  2.8 0.0 copy-start.2
  2.8 0.8 %copy-done.2 = f32[8,1024]{1,0:T(8,128)S(1)} copy-done((f32[8,1024]{1,0:T(8,128)S(1)}, f32[8,1024]{1,0:T(8,128)}, u32[]{:S(2)}) %copy-start.2) | copy-done | bytes 32792
  3.6 0.0 copy-start.3
  3.6 0.8 %copy-done.3 = f32[8,1024]{1,0:T(8,128)S(1)} copy-done((f32[8,1024]{1,0:T(8,128)S(1)}, f32[8,1024]{1,0:T(8,128)}, u32[]{:S(2)}) %copy-start.3) | copy-done | bytes 32792
  4.3 0.0 copy-start.4
  4.3 0.7 %copy-done.4 = s32[512]{0:T(512)S(1)} copy-done((s32[512]{0:T(512)S(1)}, s32[512]{0:T(512)}, u32[]{:S(2)}) %copy-start.4) | copy-done | bytes 2072
  5.0 0.0 copy-start.5
  5.0 0.7 %copy-done.5 = f32[4096]{0:T(1024)S(1)} copy-done((f32[4096]{0:T(1024)S(1)}, f32[4096]{0:T(1024)}, u32[]{:S(2)}) %copy-start.5) | copy-done | bytes 16408
  5.7 21.2 %exchange.1 = (f32[8,1024]{1,0:T(8,128)S(1)}, f32[1,128]{1,0:T(1,128)S(1)}, f32[512,128]{1,0:T(8,128)S(1)}, f32[512,128]{1,0:T(8,128)S(1)}, f32[4096,128]{1,0:T(...) custom-call(f32[4,2,2,2,8,1024]{5,4,3,2,1,0:T(8,128)S(1)} %bitcast.4, ...), custom_call_target="tpu_custom_call" | custom-call | tf_op jit(solution)/shard_map/exchange/pallas_call | solution.py:302
  26.9 3.3 %update.1 = (f32[4096,128]{1,0:T(8,128)S(1)}, f32[4096,128]{1,0:T(8,128)}, f32[8,1024]{1,0:T(8,128)}, f32[8,1024]{1,0:T(8,128)}, f32[32,128]{1,0:T(8,128)}) custom-call(f32[4096,128]{1,0:T(8,128)S(1)} %get-tuple-element.17.table, s32[512]{0:T(512)S(1)} %copy-done.4, s32[4,128]{1,0:T(4,128)S(1)} %bitcast.5, ...), custom_call_target="tpu_custom_call", output_to_operand_aliasing={{0}: (0, {})} | custom-call | tf_op jit(solution)/shard_map/update/pallas_call | solution.py:333
Async XLA Ops:
  0.6 1.2 %copy-start = (f32[1,256,1024]{2,1,0:T(8,128)S(1)}, f32[1,256,1024]{2,1,0:T(8,128)}, u32[]{:S(2)}) copy-start(f32[1,256,1024]{2,1,0:T(8,128)} %param.7) | copy-start | bytes 3145732
  1.9 0.9 %copy-start.1 = (f32[512,128]{1,0:T(8,128)S(1)}, f32[512,128]{1,0:T(8,128)}, u32[]{:S(2)}) copy-start(f32[512,128]{1,0:T(8,128)} %emb_hbm.1) | copy-start | bytes 786436
  2.8 0.8 %copy-start.2 = (f32[8,1024]{1,0:T(8,128)S(1)}, f32[8,1024]{1,0:T(8,128)}, u32[]{:S(2)}) copy-start(f32[8,1024]{1,0:T(8,128)} %param_hbm.1) | copy-start | bytes 98308
  3.6 0.8 %copy-start.3 = (f32[8,1024]{1,0:T(8,128)S(1)}, f32[8,1024]{1,0:T(8,128)}, u32[]{:S(2)}) copy-start(f32[8,1024]{1,0:T(8,128)} %dense_acc_hbm.1) | copy-start | bytes 98308
  4.3 0.7 %copy-start.4 = (s32[512]{0:T(512)S(1)}, s32[512]{0:T(512)}, u32[]{:S(2)}) copy-start(s32[512]{0:T(512)} %touched.1) | copy-start | bytes 6148
  5.0 0.7 %copy-start.5 = (f32[4096]{0:T(1024)S(1)}, f32[4096]{0:T(1024)}, u32[]{:S(2)}) copy-start(f32[4096]{0:T(1024)} %param.11) | copy-start | bytes 49156

commit v3 on v2

--- a/solution.py
+++ b/solution.py
@@ -304,7 +304,7 @@
         name="exchange",
         out_shape=(block, jax.ShapeDtypeStruct((1, LANES), f32), per_row, per_row)
         + tuple(jax.ShapeDtypeStruct(a.shape, f32) for a in own),
-        in_specs=[hbm] * 7,
+        in_specs=[pl.BlockSpec(memory_space=pltpu.HBM)] * 7,
         out_specs=(vmem,) * 9,
         scratch_shapes=[
             pltpu.VMEM((slows, fasts, ys, cores, rows, wide), f32),
@@ -329,7 +329,7 @@
         compiler_params=pltpu.CompilerParams(
             collective_id=0, has_side_effects=True, vmem_limit_bytes=49 << 20
         ),
-    )(grads, emb_grads, racc, touched, table, dense_param, dense_acc)
+    )(*[pltpu.with_memory_space_constraint(a, pltpu.HBM) for a in (grads, emb_grads, racc, touched, table, dense_param, dense_acc)])
     _, new_table, new_dense, new_dense_acc, new_racc = pl.pallas_call(
         update,
         name="update",

time: 30.7 us -> 25.2 us (0.82)
  local copies, waits for them, and re-layouts: 5.08 us -> 0.01 us
    unnamed x12 -> x2, local copies, waits for them, and re-layouts: 5.08 us -> 0.01 us
where the time goes in v3:
time: 25.2 us; the launch traced here: 25 us
  Pallas kernels  24.4 us (97%)
  between operations  0.66 us (3%)
    pallas_call x1, Pallas kernels, body(): pl.pallas_call(functools.partial(exchange, dims), name='exchange', out_sh...  21.1 us
    pallas_call x1, Pallas kernels, body(): pl.pallas_call(update, name='update', out_shape=(jax.ShapeDtypeStruct(tab...  3.34 us

profile of v3, /device:TPU:0, one launch (start us, length us, event | category | flops | bytes accessed | tf_op | source)
XLA Modules:
  0.0 25.0 jit_solution(4535992641666910285)
XLA Ops:
  0.6 0.0 copy-start
  0.6 21.1 %exchange.1 = (f32[8,1024]{1,0:T(8,128)S(1)}, f32[1,128]{1,0:T(1,128)S(1)}, f32[512,128]{1,0:T(8,128)S(1)}, f32[512,128]{1,0:T(8,128)S(1)}, f32[4096,128]{1,0:T(...) custom-call(f32[4,2,2,2,8,1024]{5,4,3,2,1,0:T(8,128)} %bitcast.5, ...), custom_call_target="tpu_custom_call" | custom-call | tf_op jit(solution)/shard_map/exchange/pallas_call | solution.py:302
  21.7 0.0 copy-done
  21.7 3.3 %update.1 = (f32[4096,128]{1,0:T(8,128)S(1)}, f32[4096,128]{1,0:T(8,128)}, f32[8,1024]{1,0:T(8,128)}, f32[8,1024]{1,0:T(8,128)}, f32[32,128]{1,0:T(8,128)}) custom-call(f32[4096,128]{1,0:T(8,128)S(1)} %get-tuple-element.17.table, s32[512]{0:T(512)S(1)} %copy-done, s32[4,128]{1,0:T(4,128)S(1)} %bitcast.4, ...), custom_call_target="tpu_custom_call", output_to_operand_aliasing={{0}: (0, {})} | custom-call | tf_op jit(solution)/shard_map/update/pallas_call | solution.py:333
Async XLA Ops:
  0.6 21.1 %copy-start = (s32[512]{0:T(512)S(1)}, s32[512]{0:T(512)}, u32[]{:S(2)}) copy-start(s32[512]{0:T(512)} %touched.1) | copy-start | bytes 6148

commit v4 on v3

--- a/solution.py
+++ b/solution.py
@@ -74,19 +74,6 @@
     for k in order:
         loads[k] = pltpu.make_async_copy(grads.at[flip(slow, k, slows)], own.at[k], load_sem.at[k])
         loads[k].start()
-    sides = []
-    held = (
-        (touched_hbm, touched),
-        (racc_hbm, racc),
-        (emb_hbm, emb),
-        (param_hbm, param_out),
-        (dense_acc_hbm, dense_acc_out),
-        (table_hbm, table_out),
-    )
-    for n, (source, target) in enumerate(held):
-        sides.append(pltpu.make_async_copy(source, target, side_sem.at[n]))
-        sides[-1].start()
-
     barrier = pltpu.get_barrier_semaphore()
     greet = [(gx, y * cores + other)]
     for a, b in plane:
@@ -109,6 +96,19 @@
             device_id_type=MESH,
         )
         pair[k].start()
+
+    sides = []
+    held = (
+        (emb_hbm, emb),
+        (touched_hbm, touched),
+        (racc_hbm, racc),
+        (param_hbm, param_out),
+        (dense_acc_hbm, dense_acc_out),
+        (table_hbm, table_out),
+    )
+    for n, (source, target) in enumerate(held):
+        sides.append(pltpu.make_async_copy(source, target, side_sem.at[n]))
+        sides[-1].start()
 
     across = {}
     for k in order:
@@ -129,20 +129,7 @@
             )
             across[k, q].start()
 
-    for side in sides[:3]:
-        side.wait()
-    lane = lax.broadcasted_iota(jnp.int32, (1, LANES), 1)
-
-    def gather(step, carry):
-        for i in range(UNROLL):
-            t = step * UNROLL + i
-            row = touched[t]
-            here = lane == row % LANES
-            lane_out[pl.ds(t, 1), :] = jnp.where(here, 1.0, 0.0)
-            acc_out[pl.ds(t, 1), :] = jnp.where(here, racc[pl.ds(row // LANES, 1), :], 0.0)
-        return carry
-
-    lax.fori_loop(0, touched.shape[0] // UNROLL, gather, 0)
+    sides[0].wait()
     values = emb[...]
     emb_square = jnp.sum(values * values, axis=0, keepdims=True)
 
@@ -193,6 +180,25 @@
             )
         )
         spread[-1].start()
+    for side in sides[1:3]:
+        side.wait()
+    lane = lax.broadcasted_iota(jnp.int32, (1, LANES), 1)
+
+    def gather(step, carry):
+        for i in range(UNROLL):
+            t = step * UNROLL + i
+            row = touched[t]
+            here = lane == row % LANES
+            lane_out[pl.ds(t, 1), :] = jnp.where(here, 1.0, 0.0)
+            acc_out[pl.ds(t, 1), :] = jnp.where(here, racc[pl.ds(row // LANES, 1), :], 0.0)
+        return carry
+
+    lax.fori_loop(0, touched.shape[0] // UNROLL, gather, 0)
+    for start in range(0, touched.shape[0], LANES):
+        part = pl.ds(start, LANES)
+        found = jnp.sum(acc_out[part, :], axis=1, keepdims=True)
+        acc_out[part, :] = jnp.broadcast_to(found, (LANES, LANES))
+
     everyone = pltpu.make_async_copy(
         norms.at[pl.ds(1, shards - 1)], norms.at[pl.ds(1, shards - 1)], norm_sem
     )
@@ -230,6 +236,7 @@
     new_dense_acc,
     new_racc,
     change,
+    placed,
     dense_v,
     acc_v,
     racc_v,
@@ -238,38 +245,43 @@
     clip = clip_ref[:, :1]
     count, width = emb.shape
 
-    def prepare(step, carry):
-        part = pl.ds(pl.multiple_of(step * LANES, LANES), LANES)
+    def prepare(start):
+        part = pl.ds(start, LANES)
         row_grads = clip * emb[part, :]
         square_mean = jnp.sum(row_grads * row_grads, axis=1, keepdims=True) / jnp.float32(width)
-        updated_acc = jnp.sum(acc_at[part, :], axis=1, keepdims=True) + square_mean
+        updated_acc = acc_at[part, :] + square_mean
         change[part, :] = learn_rate * row_grads / (jnp.sqrt(updated_acc) + epsilon)
-        placed = lane_hot[part, :] * square_mean
-        hot = jnp.where(groups == touched_rows[pl.ds(step, 1), :] // LANES, 1.0, 0.0)
-        racc_v[...] += jnp.dot(
-            hot,
-            placed,
+        placed[part, :] = lane_hot[part, :] * square_mean
+
+    def scatter(start):
+        for base in range(start, start + LANES, UNROLL):
+            rows = [touched[base + i] for i in range(UNROLL)]
+            fresh = [
+                held[pl.ds(rows[i], 1), :] - change[pl.ds(base + i, 1), :] for i in range(UNROLL)
+            ]
+            for i in range(UNROLL):
+                held[pl.ds(rows[i], 1), :] = fresh[i]
+
+    starts = range(0, count, LANES)
+    prepare(0)
+    for start in starts:
+        if start + LANES < count:
+            prepare(start + LANES)
+        scatter(start)
+    stores = [pltpu.make_async_copy(held, new_table, sems.at[0])]
+    stores[0].start()
+
+    groups = lax.broadcasted_iota(jnp.int32, racc.shape, 0)
+    added = racc[...]
+    for start in starts:
+        rows = touched_rows[start // LANES : start // LANES + 1, :]
+        added = added + jnp.dot(
+            jnp.where(groups == rows // LANES, 1.0, 0.0),
+            placed[start : start + LANES, :],
             precision=lax.Precision.HIGHEST,
             preferred_element_type=jnp.float32,
         )
-        return carry
-
-    groups = lax.broadcasted_iota(jnp.int32, racc.shape, 0)
-    racc_v[...] = racc[...]
-    for step in range(count // LANES):
-        prepare(step, 0)
-    def scatter(step, carry):
-        base = step * UNROLL
-        rows = [touched[base + i] for i in range(UNROLL)]
-        fresh = [held[pl.ds(rows[i], 1), :] - change[pl.ds(base + i, 1), :] for i in range(UNROLL)]
-        for i in range(UNROLL):
-            held[pl.ds(rows[i], 1), :] = fresh[i]
-        return carry
-
-    lax.fori_loop(0, touched.shape[0] // UNROLL, scatter, 0)
-    stores = [pltpu.make_async_copy(held, new_table, sems.at[0])]
-    stores[0].start()
-
+    racc_v[...] = added
     scaled = clip * mean[...]
     acc = dense_acc[...] + scaled * scaled
     acc_v[...] = acc
@@ -345,6 +357,7 @@
         input_output_aliases={0: 0},
         scratch_shapes=[
             pltpu.VMEM((count, width), f32),
+            pltpu.VMEM((count, LANES), f32),
             pltpu.VMEM((rows, wide), f32),
             pltpu.VMEM((rows, wide), f32),
             pltpu.VMEM(racc.shape, f32),

time: 25.2 us -> 24.2 us (0.960)
  Pallas kernels: 24.4 us -> 23.4 us
    pallas_call x1, Pallas kernels: 3.34 us -> 2.77 us  [body(): pl.pallas_call(update, name='update', out_shape=(jax.ShapeDtypeStruct(tab...]
    pallas_call x1, Pallas kernels: 21.1 us -> 20.6 us  [body(): pl.pallas_call(functools.partial(exchange, dims), name='exchange', out_sh...]
where the time goes in v4:
time: 24.2 us; the launch traced here: 24 us
  Pallas kernels  23.4 us (97%)
  between operations  0.66 us (3%)
    pallas_call x1, Pallas kernels, body(): pl.pallas_call(functools.partial(exchange, dims), name='exchange', out_sh...  20.6 us
    pallas_call x1, Pallas kernels, body(): pl.pallas_call(update, name='update', out_shape=(jax.ShapeDtypeStruct(tab...  2.77 us

profile of v4, /device:TPU:0, one launch (start us, length us, event | category | flops | bytes accessed | tf_op | source)
XLA Modules:
  0.0 24.0 jit_solution(2663612418498897730)
XLA Ops:
  0.6 0.0 copy-start
  0.6 20.6 %exchange.1 = (f32[8,1024]{1,0:T(8,128)S(1)}, f32[1,128]{1,0:T(1,128)S(1)}, f32[512,128]{1,0:T(8,128)S(1)}, f32[512,128]{1,0:T(8,128)S(1)}, f32[4096,128]{1,0:T(...) custom-call(f32[4,2,2,2,8,1024]{5,4,3,2,1,0:T(8,128)} %bitcast.5, ...), custom_call_target="tpu_custom_call" | custom-call | tf_op jit(solution)/shard_map/exchange/pallas_call | solution.py:314
  21.3 0.0 copy-done
  21.3 2.8 %update.1 = (f32[4096,128]{1,0:T(8,128)S(1)}, f32[4096,128]{1,0:T(8,128)}, f32[8,1024]{1,0:T(8,128)}, f32[8,1024]{1,0:T(8,128)}, f32[32,128]{1,0:T(8,128)}) custom-call(f32[4096,128]{1,0:T(8,128)S(1)} %get-tuple-element.17.table, s32[512]{0:T(512)S(1)} %copy-done, s32[4,128]{1,0:T(4,128)S(1)} %bitcast.4, ...), custom_call_target="tpu_custom_call", output_to_operand_aliasing={{0}: (0, {})} | custom-call | tf_op jit(solution)/shard_map/update/pallas_call | solution.py:345
Async XLA Ops:
  0.6 20.6 %copy-start = (s32[512]{0:T(512)S(1)}, s32[512]{0:T(512)}, u32[]{:S(2)}) copy-start(s32[512]{0:T(512)} %touched.1) | copy-start | bytes 6148

commit v5 on v4

--- a/solution.py
+++ b/solution.py
@@ -220,7 +220,7 @@
 
 def update(
     table,
-    touched,
+    touched_any,
     touched_rows,
     clip_ref,
     mean,
@@ -240,8 +240,11 @@
     dense_v,
     acc_v,
     racc_v,
+    touched,
     sems,
 ):
+    numbers = pltpu.make_async_copy(touched_any, touched, sems.at[4])
+    numbers.start()
     clip = clip_ref[:, :1]
     count, width = emb.shape
 
@@ -263,13 +266,27 @@
                 held[pl.ds(rows[i], 1), :] = fresh[i]
 
     starts = range(0, count, LANES)
-    prepare(0)
+    ahead = 2
+    for start in starts[:ahead]:
+        prepare(start)
+    numbers.wait()
     for start in starts:
-        if start + LANES < count:
-            prepare(start + LANES)
+        if start + ahead * LANES < count:
+            prepare(start + ahead * LANES)
         scatter(start)
     stores = [pltpu.make_async_copy(held, new_table, sems.at[0])]
     stores[0].start()
+
+    def send(n, source, target):
+        stores.append(pltpu.make_async_copy(source, target, sems.at[n]))
+        stores[-1].start()
+
+    scaled = clip * mean[...]
+    acc = dense_acc[...] + scaled * scaled
+    acc_v[...] = acc
+    dense_v[...] = dense_param[...] - learn_rate * scaled / (jnp.sqrt(acc) + epsilon)
+    send(1, acc_v, new_dense_acc)
+    send(2, dense_v, new_dense)
 
     groups = lax.broadcasted_iota(jnp.int32, racc.shape, 0)
     added = racc[...]
@@ -282,14 +299,7 @@
             preferred_element_type=jnp.float32,
         )
     racc_v[...] = added
-    scaled = clip * mean[...]
-    acc = dense_acc[...] + scaled * scaled
-    acc_v[...] = acc
-    dense_v[...] = dense_param[...] - learn_rate * scaled / (jnp.sqrt(acc) + epsilon)
-    pairs = ((racc_v, new_racc), (acc_v, new_dense_acc), (dense_v, new_dense))
-    for n, (source, target) in enumerate(pairs):
-        stores.append(pltpu.make_async_copy(source, target, sems.at[n + 1]))
-        stores[-1].start()
+    send(3, racc_v, new_racc)
     for store in stores:
         store.wait()
 
@@ -304,7 +314,6 @@
     racc = row_acc.reshape(-1, LANES)
     touched_rows = touched.reshape(-1, LANES)
     vmem = pl.BlockSpec(memory_space=pltpu.VMEM)
-    smem = pl.BlockSpec(memory_space=pltpu.SMEM)
     hbm = pl.BlockSpec(memory_space=pl.ANY)
     quad = fasts * ys
     dma = pltpu.SemaphoreType.DMA
@@ -352,7 +361,7 @@
             block,
             jax.ShapeDtypeStruct(racc.shape, f32),
         ),
-        in_specs=[vmem, smem] + [vmem] * 9,
+        in_specs=[vmem, hbm] + [vmem] * 9,
         out_specs=(vmem,) + (hbm,) * 4,
         input_output_aliases={0: 0},
         scratch_shapes=[
@@ -361,7 +370,8 @@
             pltpu.VMEM((rows, wide), f32),
             pltpu.VMEM((rows, wide), f32),
             pltpu.VMEM(racc.shape, f32),
-            dma((4,)),
+            pltpu.SMEM((count,), jnp.int32),
+            dma((5,)),
         ],
         compiler_params=pltpu.CompilerParams(
             vmem_limit_bytes=2 * table.size * 4 + 8 * count * LANES * 4 + (4 << 20)

time: 24.2 us -> 24 us (level)
  no operation moved by 1% of the time
where the time goes in v5:
time: 24 us; the launch traced here: 23.9 us
  Pallas kernels  23.2 us (97%)
  between operations  0.66 us (3%)
    pallas_call x1, Pallas kernels, body(): pl.pallas_call(functools.partial(exchange, dims), name='exchange', out_sh...  20.6 us
    pallas_call x1, Pallas kernels, body(): pl.pallas_call(update, name='update', out_shape=(jax.ShapeDtypeStruct(tab...  2.6 us

profile of v5, /device:TPU:0, one launch (start us, length us, event | category | flops | bytes accessed | tf_op | source)
XLA Modules:
  0.0 23.9 jit_solution(4106752281674344855)
XLA Ops:
  0.6 0.0 copy-start
  0.6 20.6 %exchange.1 = (f32[8,1024]{1,0:T(8,128)S(1)}, f32[1,128]{1,0:T(1,128)S(1)}, f32[512,128]{1,0:T(8,128)S(1)}, f32[512,128]{1,0:T(8,128)S(1)}, f32[4096,128]{1,0:T(...) custom-call(f32[4,2,2,2,8,1024]{5,4,3,2,1,0:T(8,128)} %bitcast.5, ...), custom_call_target="tpu_custom_call" | custom-call | tf_op jit(solution)/shard_map/exchange/pallas_call | solution.py:323
  21.3 0.0 copy-done
  21.3 2.6 %update.1 = (f32[4096,128]{1,0:T(8,128)S(1)}, f32[4096,128]{1,0:T(8,128)}, f32[8,1024]{1,0:T(8,128)}, f32[8,1024]{1,0:T(8,128)}, f32[32,128]{1,0:T(8,128)}) custom-call(f32[4096,128]{1,0:T(8,128)S(1)} %get-tuple-element.17.table, s32[512]{0:T(512)S(1)} %copy-done, s32[4,128]{1,0:T(4,128)S(1)} %bitcast.4, ...), custom_call_target="tpu_custom_call", output_to_operand_aliasing={{0}: (0, {})} | custom-call | tf_op jit(solution)/shard_map/update/pallas_call | solution.py:354
Async XLA Ops:
  0.6 20.6 %copy-start = (s32[512]{0:T(512)S(1)}, s32[512]{0:T(512)}, u32[]{:S(2)}) copy-start(s32[512]{0:T(512)} %touched_any.1) | copy-start | bytes 6148

commit v6 on v5

--- a/solution.py
+++ b/solution.py
@@ -71,9 +71,12 @@
     order = list(reversed(range(slows)))
 
     loads = {}
-    for k in order:
-        loads[k] = pltpu.make_async_copy(grads.at[flip(slow, k, slows)], own.at[k], load_sem.at[k])
-        loads[k].start()
+    for half, who in enumerate((other, core)):
+        for k in order:
+            loads[k, half] = pltpu.make_async_copy(
+                grads.at[flip(slow, k, slows), :, :, who], own.at[k, :, :, who], load_sem.at[k, half]
+            )
+            loads[k, half].start()
     barrier = pltpu.get_barrier_semaphore()
     greet = [(gx, y * cores + other)]
     for a, b in plane:
@@ -86,7 +89,7 @@
 
     pair = {}
     for k in order:
-        loads[k].wait()
+        loads[k, 0].wait()
         pair[k] = pltpu.make_async_remote_copy(
             src_ref=own.at[k, :, :, other],
             dst_ref=pair_in.at[k],
@@ -112,6 +115,7 @@
 
     across = {}
     for k in order:
+        loads[k, 1].wait()
         pair[k].wait_recv()
         for a in range(fasts):
             for b in range(ys):
@@ -336,7 +340,7 @@
             pltpu.VMEM((slows, rows, wide), f32),
             pltpu.VMEM((shards, 1, LANES), f32),
             pltpu.SMEM((count,), jnp.int32),
-            dma((slows,)),
+            dma((slows, 2)),
             dma((slows,)),
             dma((slows,)),
             dma((slows, quad)),

time: 24 us -> 24.1 us (level)
  no operation moved by 1% of the time
where the time goes in v6:
time: 24.1 us; the launch traced here: 23.9 us
  Pallas kernels  23.3 us (97%)
  between operations  0.66 us (3%)
    pallas_call x1, Pallas kernels, body(): pl.pallas_call(functools.partial(exchange, dims), name='exchange', out_sh...  20.7 us
    pallas_call x1, Pallas kernels, body(): pl.pallas_call(update, name='update', out_shape=(jax.ShapeDtypeStruct(tab...  2.6 us

profile of v6, /device:TPU:0, one launch (start us, length us, event | category | flops | bytes accessed | tf_op | source)
XLA Modules:
  0.0 23.9 jit_solution(17221686064790623163)
XLA Ops:
  0.6 0.0 copy-start
  0.6 20.7 %exchange.1 = (f32[8,1024]{1,0:T(8,128)S(1)}, f32[1,128]{1,0:T(1,128)S(1)}, f32[512,128]{1,0:T(8,128)S(1)}, f32[512,128]{1,0:T(8,128)S(1)}, f32[4096,128]{1,0:T(...) custom-call(f32[4,2,2,2,8,1024]{5,4,3,2,1,0:T(8,128)} %bitcast.5, ...), custom_call_target="tpu_custom_call" | custom-call | tf_op jit(solution)/shard_map/exchange/pallas_call | solution.py:327
  21.3 0.0 copy-done
  21.3 2.6 %update.1 = (f32[4096,128]{1,0:T(8,128)S(1)}, f32[4096,128]{1,0:T(8,128)}, f32[8,1024]{1,0:T(8,128)}, f32[8,1024]{1,0:T(8,128)}, f32[32,128]{1,0:T(8,128)}) custom-call(f32[4096,128]{1,0:T(8,128)S(1)} %get-tuple-element.17.table, s32[512]{0:T(512)S(1)} %copy-done, s32[4,128]{1,0:T(4,128)S(1)} %bitcast.4, ...), custom_call_target="tpu_custom_call", output_to_operand_aliasing={{0}: (0, {})} | custom-call | tf_op jit(solution)/shard_map/update/pallas_call | solution.py:358
Async XLA Ops:
  0.6 20.7 %copy-start = (s32[512]{0:T(512)S(1)}, s32[512]{0:T(512)}, u32[]{:S(2)}) copy-start(s32[512]{0:T(512)} %touched_any.1) | copy-start | bytes 6148
